TPU v7x, 32 devices: a whole 2x2x4 slice. The times are simulated.
32 devices in a mesh: gx: 4 (over x, core), gy: 4 (over z), gz: 2 (over y).
Axes of the slice: x: 2, y: 2, z: 4, core: 2. Of those that a mesh axis runs over, the one named last changes fastest.
Arguments:
- in_first: bfloat16 [16384, 1024], P(('gx', 'gy', 'gz')), may hold values from -98 to 98
- cot_first: bfloat16 [16384, 256], P(('gx', 'gy', 'gz')), may hold values from -0.234375 to 0.234375
- in_third: bfloat16 [16384, 256], P(('gx', 'gy', 'gz')), may hold values from -98 to 98
- cot_third: bfloat16 [16384, 1024], P(('gx', 'gy', 'gz')), may hold values from -0.234375 to 0.234375
- mean_old: float32 [524288], P(('gx', 'gy', 'gz')), may hold values from -6 to 6
- prec_old: float32 [524288], P(('gx', 'gy', 'gz')), may hold values from 0.5 to 4
- mom_old: float32 [524288], P(('gx', 'gy', 'gz')), may hold values from -4 to 4
- noise: bfloat16 [32, 524288], P(('gx', 'gy', 'gz')), may hold values from -6 to 6
Outputs:
- mean_new: float32 [524288], P(('gx', 'gy', 'gz'))
- prec_new: float32 [524288], P(('gx', 'gy', 'gz'))
- mom_new: float32 [524288], P(('gx', 'gy', 'gz'))
- samples: bfloat16 [32, 524288], P(('gx', 'gy', 'gz'))
All inputs are finite; a program needn't handle non-finite values.
Results may differ from a plain program's by a relative error of at most 0.0016.
Values sent between devices are 32-bit elements; how exact they have to be, the bound alone decides.
A program may use at most 64 MiB of HBM per device.

v0:
```python
import jax
import jax.numpy as jnp
from jax import lax
from jax.sharding import PartitionSpec as P


def squared(values):
    wide = values.astype(jnp.float32)
    return (wide * wide).astype(jnp.bfloat16)


def contract_rows(left, right):
    return lax.dot_general(
        left, right, (((0,), (0,)), ((), ())), preferred_element_type=jnp.float32
    )


def on_device(in_first, cot_first, in_third, cot_third, mean_old, prec_old, mom_old, noise):
    grad_first = contract_rows(in_first, cot_first)
    grad_third = contract_rows(in_third, cot_third)
    curv_first = contract_rows(squared(in_first), squared(cot_first))
    curv_third = contract_rows(squared(in_third), squared(cot_third))
    grad_flat = jnp.concatenate([grad_first.reshape(-1), grad_third.reshape(-1)])
    curv_flat = jnp.concatenate([curv_first.reshape(-1), curv_third.reshape(-1)])
    grad, curv = (
        lax.psum_scatter(grad_flat, ("gx", "gy", "gz"), scatter_dimension=0, tiled=True),
        lax.psum_scatter(curv_flat, ("gx", "gy", "gz"), scatter_dimension=0, tiled=True),
    )
    prec_new = 0.5 * prec_old + 0.5 * curv
    mom_new = 0.9 * mom_old + grad + 0.1 * mean_old
    divisor = prec_new + 0.1 + 0.05
    mean_new = mean_old - 0.3 * mom_new / divisor
    spread = jnp.sqrt(0.3 / divisor)
    posterior = jnp.stack([mean_new, spread])
    noise_row = noise[0]
    piece = lax.all_gather(posterior, ("gx", "gy", "gz"), axis=1, tiled=True)
    normal = noise_row.astype(jnp.float32)
    sample_row = (piece[0] + piece[1] * normal).astype(jnp.bfloat16)
    return (mean_new, prec_new, mom_new, sample_row.reshape(1, -1))


def solution(mesh):
    placed = (
        P(("gx", "gy", "gz"), None),
        P(("gx", "gy", "gz"), None),
        P(("gx", "gy", "gz"), None),
        P(("gx", "gy", "gz"), None),
        P(("gx", "gy", "gz")),
        P(("gx", "gy", "gz")),
        P(("gx", "gy", "gz")),
        P(("gx", "gy", "gz"), None),
    )
    return jax.shard_map(
        on_device,
        mesh=mesh,
        in_specs=placed,
        out_specs=(
            P(("gx", "gy", "gz")),
            P(("gx", "gy", "gz")),
            P(("gx", "gy", "gz")),
            P(("gx", "gy", "gz"), None),
        ),
        check_vma=False,
    )
```

profile of v0, /device:TPU:1, one launch (start us, length us, event | category | flops | bytes accessed | tf_op | source)
XLA Modules:
  0.0 239.3 jit_solution(8979160282534299743)
XLA Ops:
  7.2 0.0 copy-start.3
  7.2 0.0 copy-start.4
  7.2 0.0 copy-start.2
  7.2 0.0 copy-start
  7.2 0.0 all-reduce.5.cloned.1.call-start
  7.3 1.9 convolution_bitcast_fusion.3
  9.1 0.0 copy-done.3
  9.2 0.0 copy-done.4
  9.2 0.5 convolution_bitcast_fusion.1
  9.7 0.0 copy-done.2
  9.7 0.0 copy-done
  9.7 0.5 convolution_bitcast_fusion.2
  10.2 0.5 convolution_bitcast_fusion
  10.6 0.5 copy.12
  11.2 0.2 copy.13
  11.4 0.5 copy.14
  11.9 0.2 copy.15
  12.2 2.3 pad_maximum_fusion
  14.5 0.0 copy-start.7
  14.5 0.0 copy-start.8
  14.5 0.0 copy-start.9
  14.5 0.0 copy-start.1
  14.5 0.0 all-reduce.5.cloned.1.call-update
  14.5 0.0 all-gather.2.cloned.1.call-start
  14.6 143.0 %all-reduce.5.cloned.1.call-done = (f32[524288]{0:T(1024)}, f32[524288]{0:T(1024)}) async-done(((f32[524288]{0:T(1024)}, f32[524288]{0:T(1024)}), (f32[524288]{0:T(1024)}, f32[524288]{0:T(1024)})) %all-reduce.5.cloned.1.call-update) | async-done | bytes 4194320
  157.5 0.0 copy-done.7
  157.5 0.9 divide_sqrt_fusion
  158.4 0.0 copy-start.5
  158.4 0.0 copy-done.8
  158.4 0.0 copy-done.9
  158.4 1.5 divide_subtract_fusion
  159.9 0.0 copy-start.6
  159.9 0.8 pad_maximum_fusion.2
  160.7 0.0 all-gather.2.cloned.1.call-update
  160.7 63.5 %all-gather.2.cloned.1.call-done = f32[2,524288]{1,0:T(2,128)} async-done(((f32[2,16384]{1,0:T(2,128)}), f32[2,524288]{1,0:T(2,128)}) %all-gather.2.cloned.1.call-update) | async-done | bytes 4194320 | tf_op jit(solution)/shard_map/all_gather | solution.py:36
  224.3 0.0 copy-done.1
  224.3 8.2 %fusion.1 = bf16[1,524288]{1,0:T(2,128)(2,1)} fusion(bf16[1,524288]{1,0:T(2,128)(2,1)S(1)} %copy-done.1, f32[2,524288]{1,0:T(2,128)} %all-gather.2.cloned.1.call-done), kind=kLoop, calls=%fused_computation.6 | loop fusion | flops 2097152 | bytes 6291456 | tf_op jit(solution)/shard_map/convert_element_type | solution.py:38
  232.4 0.0 copy-done.5
  232.4 0.0 copy-done.6
Async XLA Ops:
  7.2 2.0 copy-start.3
  7.2 2.0 copy-start.4
  7.2 2.5 %copy-start.2 = (bf16[512,256]{1,0:T(8,128)(2,1)S(1)}, bf16[512,256]{1,0:T(8,128)(2,1)}, u32[]{:S(2)}) copy-start(bf16[512,256]{1,0:T(8,128)(2,1)} %param.10) | copy-start | bytes 786436
  7.2 2.5 %copy-start = (bf16[512,1024]{1,0:T(8,128)(2,1)S(1)}, bf16[512,1024]{1,0:T(8,128)(2,1)}, u32[]{:S(2)}) copy-start(bf16[512,1024]{1,0:T(8,128)(2,1)} %param.11) | copy-start | bytes 3145732
  7.2 150.3 %all-reduce.5.cloned.1.call-start = ((), (), s32[]{:S(2)}) async-start(), calls=%async_computation.1 | async-start | bytes 8388608
  14.5 143.0 %copy-start.7 = (f32[16384]{0:T(1024)S(1)}, f32[16384]{0:T(1024)}, u32[]{:S(2)}) copy-start(f32[16384]{0:T(1024)} %param.13) | copy-start | bytes 196612
  14.5 143.9 %copy-start.8 = (f32[16384]{0:T(1024)S(1)}, f32[16384]{0:T(1024)}, u32[]{:S(2)}) copy-start(f32[16384]{0:T(1024)} %param.12) | copy-start | bytes 196612
  14.5 143.9 %copy-start.9 = (f32[16384]{0:T(1024)S(1)}, f32[16384]{0:T(1024)}, u32[]{:S(2)}) copy-start(f32[16384]{0:T(1024)} %param.14) | copy-start | bytes 196612
  14.5 209.8 %copy-start.1 = (bf16[1,524288]{1,0:T(2,128)(2,1)S(1)}, bf16[1,524288]{1,0:T(2,128)(2,1)}, u32[]{:S(2)}) copy-start(bf16[1,524288]{1,0:T(2,128)(2,1)} %param.15) | copy-start | bytes 3145732
  14.5 209.7 %all-gather.2.cloned.1.call-start = ((), (), s32[]{:S(2)}) async-start(), calls=%async_computation | async-start | bytes 4325376 | tf_op jit(solution)/shard_map/all_gather | solution.py:36
  158.4 74.0 %copy-start.5 = (f32[16384]{0:T(1024)}, f32[16384]{0:T(1024)S(1)}, u32[]{:S(2)}) copy-start(f32[16384]{0:T(1024)S(1)} %get-tuple-element.7) | copy-start | bytes 196612
  159.9 72.5 %copy-start.6 = (f32[16384]{0:T(1024)}, f32[16384]{0:T(1024)S(1)}, u32[]{:S(2)}) copy-start(f32[16384]{0:T(1024)S(1)} %get-tuple-element.8) | copy-start | bytes 196612
Sparse Core Ops, SparseCore 0:
  14.6 142.8 all-reduce.4
  161.2 63.0 all-gather.1
where the time goes:
time: 240 us; the launch traced here: 239 us
  waiting for transfers between devices  207 us (86%)
  between operations  14.2 us (6%)
  other arithmetic  13.7 us (6%)
  matrix products  3.33 us (1%)
    unnamed x3, waiting for transfers between devices  143 us
    all_gather x1, waiting for transfers between devices, on_device(): piece = lax.all_gather(posterior, ('gx', 'gy', 'gz'), axis=1, tiled=True)  63.5 us
    convert_element_type x1, other arithmetic, on_device(): sample_row = (piece[0] + piece[1] * normal).astype(jnp.bfloat16)  8.18 us
  transfers between devices with their start and end apart: 2, of which 2 were waited for; matrix products, arithmetic and copies ran while one was open for 0% of the time, Pallas kernels for 0%

commit v1 on v0

v1 whole, which is shorter than its diff:
```python
import functools

import jax
import jax.numpy as jnp
from jax import lax
from jax.experimental import pallas as pl
from jax.experimental.pallas import tpu as pltpu
from jax.sharding import PartitionSpec as P

LANES = 128
BLOCK = 256
AXES = ("gx", "gy", "gz")


def squared(values):
    wide = values.astype(jnp.float32)
    return (wide * wide).astype(jnp.bfloat16)


def contract_rows(left, right):
    return lax.dot_general(
        left, right, (((0,), (0,)), ((), ())), preferred_element_type=jnp.float32
    )


def step_kernel(
    sizes,
    in_first, cot_first, in_third, cot_third, mean_old, prec_old, mom_old,
    mean_out, prec_out, mom_out, gathered,
    part, got_c, sum_f, got_f, sum_g, got_g, sum_z, got_z, divisor,
    c_sems, f_sems, g_sems, z_sems, zz_sems, gg_sems, ff_sems, cc_sems,
):
    X, C, Z, Y, S, splits = sizes
    s = S // splits
    gx, mz, my = (lax.axis_index(name) for name in AXES)
    mx, mc = gx // C, lax.rem(gx, C)
    other_c = 1 - mc

    def device(x=None, c=None, z=None, y=None):
        x = mx if x is None else x
        c = mc if c is None else c
        return (x * C + c, mz if z is None else z, my if y is None else y)

    def away(mine, step, size):
        return lax.rem(mine + step, size)

    barrier = pltpu.get_barrier_semaphore()
    peers = [device(c=other_c)]
    peers += [device(x=away(mx, k, X)) for k in range(1, X)]
    peers += [device(y=away(my, k, Y)) for k in range(1, Y)]
    peers += [device(z=away(mz, k, Z)) for k in range(1, Z)]
    for peer in peers:
        pl.semaphore_signal(barrier, inc=1, device_id=peer, device_id_type=pl.DeviceIdType.MESH)

    started = []

    def link(src, dst, sems, index, peer):
        return pltpu.make_async_remote_copy(
            src_ref=src, dst_ref=dst,
            send_sem=sems.at[(0,) + index], recv_sem=sems.at[(1,) + index],
            device_id=peer, device_id_type=pl.DeviceIdType.MESH,
        )

    def send(*args):
        copy = link(*args)
        copy.start()
        started.append(copy)

    def place(index):
        rest, y = divmod(index, Y)
        rest, z = divmod(rest, Z)
        x, c = divmod(rest, C)
        return x, c, z, y

    def put(kind, base, block, row0, col0, width):
        rows = S * LANES // width
        across = width // LANES
        for i in range(block.shape[0] // rows):
            x, c, z, y = place(base + row0 // rows + i)
            for j in range(block.shape[1] // LANES):
                part[kind, x, c, z, y, pl.ds(col0 // LANES + j, rows, stride=across), :] = (
                    block[i * rows:(i + 1) * rows, j * LANES:(j + 1) * LANES]
                )

    def products(kind, shape):
        cin, mid = in_first.shape[1], cot_first.shape[1]
        right = shape(cot_first[...])
        for r in range(0, cin, BLOCK):
            put(kind, 0, contract_rows(shape(in_first[:, r:r + BLOCK]), right), r, 0, mid)
        base = X * C * Z * Y // 2
        left = shape(in_third[...])
        for r in range(0, cin, BLOCK):
            put(kind, base, contract_rows(left, shape(cot_third[:, r:r + BLOCK])), 0, r, cin)

    pieces = [(kind, split) for kind in (0, 1) for split in range(splits)]
    flip = [(kind + split) % 2 if splits == 1 else split % 2 for kind, split in pieces]

    def rows_of(p):
        split = pieces[p][1]
        return pl.ds(split * s, s)

    def outer(p):
        return (Y, my, X, mx) if flip[p] else (X, mx, Y, my)

    def xy(p, f, g):
        return (g, f) if flip[p] else (f, g)

    def f_peer(p, f):
        return device(y=f) if flip[p] else device(x=f)

    def g_peer(p, g):
        return device(x=g) if flip[p] else device(y=g)

    def c_link(p, i):
        x = away(mx, i + 1, X)
        return (part.at[pieces[p][0], x, other_c, :, :, rows_of(p), :],
                got_c.at[p, x], c_sems, (p, i), device(c=other_c))

    def c_send(ps):
        for i in range(X):
            for p in ps:
                send(*c_link(p, i))

    def c_add(p):
        nf, mf, ng, mg = outer(p)
        for i in range(X):
            link(*c_link(p, i)).wait_recv()
        kind = pieces[p][0]
        for i in range(nf):
            f = away(mf, i + 1, nf)
            for j in range(ng):
                g = away(mg, j + 1, ng)
                x, y = xy(p, f, g)
                sum_f[p, i * ng + j] = part[kind, x, mc, :, y, rows_of(p), :] + got_c[p, x, :, y]

    def f_link(p, i, j):
        nf, mf, ng, mg = outer(p)
        slot = i * ng + j
        return (sum_f.at[p, slot], got_f.at[p, slot], f_sems, (p, slot),
                f_peer(p, away(mf, i + 1, nf)))

    def f_send(p):
        nf, mf, ng, mg = outer(p)
        for j in range(ng):
            for i in range(nf - 1):
                send(*f_link(p, i, j))

    def g_link(p, j):
        nf, mf, ng, mg = outer(p)
        return (sum_g.at[p, j], got_g.at[p, j], g_sems, (p, j),
                g_peer(p, away(mg, j + 1, ng)))

    def f_add(p, js):
        nf, mf, ng, mg = outer(p)
        for j in js:
            total = sum_f[p, (nf - 1) * ng + j]
            for i in range(nf - 1):
                link(*f_link(p, i, j)).wait_recv()
                total = total + got_f[p, i * ng + j]
            sum_g[p, j] = total
            if j < ng - 1:
                send(*g_link(p, j))

    def z_link(p, k):
        z = away(mz, k + 1, Z)
        return (sum_z.at[p, z], got_z.at[p, k], z_sems, (p, k), device(z=z))

    def g_add(p):
        nf, mf, ng, mg = outer(p)
        total = sum_g[p, ng - 1]
        for j in range(ng - 1):
            link(*g_link(p, j)).wait_recv()
            total = total + got_g[p, j]
        sum_z[p] = total
        for k in range(Z - 1):
            send(*z_link(p, k))

    def z_add(p):
        total = sum_z[p, mz]
        for k in range(Z - 1):
            link(*z_link(p, k)).wait_recv()
            total = total + got_z[p, k]
        return total

    def tile(p, x, c, z, y):
        return gathered.at[pieces[p][0], x, c, z, y, rows_of(p), :]

    def column(p, x, c, y):
        return gathered.at[pieces[p][0], x, c, :, y, rows_of(p), :]

    def zz_link(p, k, recv=False):
        z = away(mz, Z - 1 - k, Z) if recv else mz
        ref = tile(p, mx, mc, z, my)
        return (ref, ref, zz_sems, (p, k), device(z=away(mz, k + 1, Z)))

    def gg_link(p, j, k, recv=False):
        nf, mf, ng, mg = outer(p)
        g = away(mg, ng - 1 - j, ng) if recv else mg
        x, y = xy(p, mf, g)
        ref = tile(p, x, mc, away(mz, Z - k, Z), y)
        return (ref, ref, gg_sems, (p, j * Z + k), g_peer(p, away(mg, j + 1, ng)))

    def ff_link(p, i, j, recv=False):
        nf, mf, ng, mg = outer(p)
        f = away(mf, nf - 1 - i, nf) if recv else mf
        x, y = xy(p, f, away(mg, ng - j, ng))
        ref = column(p, x, mc, y)
        return (ref, ref, ff_sems, (p, i * ng + j), f_peer(p, away(mf, i + 1, nf)))

    def cc_link(p, i, j, recv=False):
        nf, mf, ng, mg = outer(p)
        x, y = xy(p, away(mf, nf - i, nf), away(mg, ng - j, ng))
        ref = column(p, x, other_c if recv else mc, y)
        return (ref, ref, cc_sems, (p, i * ng + j), device(c=other_c))

    def zz_send(p):
        nf, mf, ng, mg = outer(p)
        for k in range(Z - 1):
            send(*zz_link(p, k))
        for j in range(ng - 1):
            send(*gg_link(p, j, 0))

    def gg_send(p):
        nf, mf, ng, mg = outer(p)
        for k in range(Z - 1):
            link(*zz_link(p, k, True)).wait_recv()
            for j in range(ng - 1):
                send(*gg_link(p, j, k + 1))
        for i in range(nf - 1):
            send(*ff_link(p, i, 0))
        send(*cc_link(p, 0, 0))

    def ff_send(p):
        nf, mf, ng, mg = outer(p)
        for j in range(1, ng):
            for k in range(Z):
                link(*gg_link(p, j - 1, k, True)).wait_recv()
            for i in range(nf - 1):
                send(*ff_link(p, i, j))
            send(*cc_link(p, 0, j))

    def cc_send(p):
        nf, mf, ng, mg = outer(p)
        for j in range(ng):
            for i in range(1, nf):
                link(*ff_link(p, i - 1, j, True)).wait_recv()
                send(*cc_link(p, i, j))

    def cc_wait(p):
        nf, mf, ng, mg = outer(p)
        for i in range(nf):
            for j in range(ng):
                link(*cc_link(p, i, j, True)).wait_recv()

    def publish(p, value):
        gathered[pieces[p][0], mx, mc, mz, my, rows_of(p), :] = value
        zz_send(p)

    def own_curv(p):
        at = rows_of(p)
        prec = 0.5 * prec_old[at, :] + 0.5 * z_add(p)
        prec_out[at, :] = prec
        div = prec + 0.1 + 0.05
        divisor[at, :] = div
        publish(p, jnp.sqrt(0.3 / div))

    def own_grad(p):
        at = rows_of(p)
        mean = mean_old[at, :]
        mom = 0.9 * mom_old[at, :] + z_add(p) + 0.1 * mean
        mom_out[at, :] = mom
        new = mean - 0.3 * mom / divisor[at, :]
        mean_out[at, :] = new
        publish(p, new)

    curv = list(range(splits))
    grad = list(range(splits, 2 * splits))

    products(0, squared)
    pl.semaphore_wait(barrier, len(peers))
    c_send(curv)
    products(1, lambda values: values)
    c_send(grad)
    for p in curv:
        c_add(p)
        f_send(p)
    for p in grad:
        c_add(p)

    def halves(p):
        ng = outer(p)[2]
        return range(ng - 1), range(ng - 1, ng)

    for p in curv:
        f_add(p, halves(p)[0])
    for p in grad:
        f_send(p)
    for p in curv:
        f_add(p, halves(p)[1])
    for p in curv:
        g_add(p)
    for p in grad:
        f_add(p, halves(p)[0])
    for p in grad:
        f_add(p, halves(p)[1])
    for p in curv:
        own_curv(p)
    for p in grad:
        g_add(p)
    for p in curv:
        gg_send(p)
    for p in grad:
        own_grad(p)
    for p in curv:
        ff_send(p)
    for p in grad:
        gg_send(p)
    for p in curv:
        cc_send(p)
    for p in grad:
        ff_send(p)
    for p in grad:
        cc_send(p)
    for p in curv + grad:
        cc_wait(p)
    for copy in started:
        copy.wait_send()


def on_device(sizes, in_first, cot_first, in_third, cot_third, mean_old, prec_old, mom_old, noise):
    X, C, Z, Y, S, splits = sizes
    n, s = 2 * splits, S // splits
    shard = jax.ShapeDtypeStruct((S, LANES), jnp.float32)
    vmem = pl.BlockSpec(memory_space=pltpu.VMEM)
    wide = max(X, Y)

    def f32(*shape):
        return pltpu.VMEM(shape + (LANES,), jnp.float32)

    def sems(*shape):
        return pltpu.SemaphoreType.DMA((2, n) + shape)

    mean_new, prec_new, mom_new, both = pl.pallas_call(
        functools.partial(step_kernel, sizes),
        out_shape=(shard, shard, shard, jax.ShapeDtypeStruct((2, X, C, Z, Y, S, LANES), jnp.float32)),
        in_specs=[vmem] * 7,
        out_specs=[vmem] * 4,
        scratch_shapes=[
            f32(2, X, C, Z, Y, S),
            f32(n, X, Z, Y, s),
            f32(n, X * Y, Z, s),
            f32(n, X * Y, Z, s),
            f32(n, wide, Z, s),
            f32(n, wide, Z, s),
            f32(n, Z, s),
            f32(n, Z, s),
            f32(S),
            sems(X), sems(X * Y), sems(wide), sems(Z),
            sems(Z), sems(wide * Z), sems(X * Y), sems(X * Y),
        ],
        compiler_params=pltpu.CompilerParams(
            collective_id=0, has_side_effects=True, vmem_limit_bytes=48 * 1024 * 1024
        ),
    )(in_first, cot_first, in_third, cot_third,
      *(old.reshape(S, LANES) for old in (mean_old, prec_old, mom_old)))
    spread, mean = both[0].reshape(-1), both[1].reshape(-1)
    sample_row = (mean + spread * noise[0].astype(jnp.float32)).astype(jnp.bfloat16)
    return (mean_new.reshape(-1), prec_new.reshape(-1), mom_new.reshape(-1), sample_row.reshape(1, -1))


def solution(mesh):
    GX, GY, GZ = (mesh.shape[name] for name in AXES)
    split = P(AXES)
    rows = P(AXES, None)

    def whole_step(*arrays):
        params = arrays[4].shape[0]
        S = params // (GX * GY * GZ) // LANES
        sizes = (GX // 2, 2, GY, GZ, S, 2 if S % 16 == 0 else 1)
        return jax.shard_map(
            functools.partial(on_device, sizes),
            mesh=mesh,
            in_specs=(rows, rows, rows, rows, split, split, split, rows),
            out_specs=(split, split, split, rows),
            check_vma=False,
        )(*arrays)

    return whole_step
```

time: 240 us -> 73.9 us (0.31)
  waiting for transfers between devices: 207 us -> 0 us
  Pallas kernels: 0 us -> 56.8 us
  between operations: 14.2 us -> 0.67 us
  local copies, waits for them, and re-layouts: 1.52 us -> 11.6 us
  other arithmetic: 13.7 us -> 4.44 us
  matrix products: 3.33 us -> 0 us
    unnamed x3 -> x0, waiting for transfers between devices: 143 us -> none
    all_gather x1 -> x0, waiting for transfers between devices: 63.5 us -> none  [on_device(): piece = lax.all_gather(posterior, ('gx', 'gy', 'gz'), axis=1, tiled=True)]
    pallas_call x0 -> x1, Pallas kernels: none -> 56.8 us  [on_device(): pl.pallas_call(functools.partial(step_kernel, sizes), out_shape=(shard, s...]
    unnamed x24 -> x19, local copies, waits for them, and re-layouts: 1.52 us -> 8.96 us
    convert_element_type x1, other arithmetic: 8.18 us -> 4.44 us  [on_device(): (mean + spread * noise[0].astype(jnp.float32)).astype(jnp.bfloat16)]
    dot_general x4 -> x0, matrix products: 3.33 us -> none  [contract_rows(): lax.dot_general(left, right, (((0,), (0,)), ((), ())), preferred_element_...]
    slice x0 -> x1, local copies, waits for them, and re-layouts: none -> 2.64 us  [on_device(): spread, mean = (both[0].reshape(-1), both[1].reshape(-1))]
  transfers between devices with their start and end apart: 2 -> 0, of which waited for: 2 -> 0; matrix products, arithmetic and copies ran while one was open for 0% -> 0% of each run, Pallas kernels for 0% -> 0%
where the time goes in v1:
time: 73.9 us; the launch traced here: 73.5 us
  Pallas kernels  56.8 us (77%)
  local copies, waits for them, and re-layouts  11.6 us (16%)
  other arithmetic  4.44 us (6%)
    pallas_call x1, Pallas kernels, on_device(): pl.pallas_call(functools.partial(step_kernel, sizes), out_shape=(shard, s...  56.8 us
    unnamed x19, local copies, waits for them, and re-layouts  8.96 us
    convert_element_type x1, other arithmetic, on_device(): (mean + spread * noise[0].astype(jnp.float32)).astype(jnp.bfloat16)  4.44 us
    slice x1, local copies, waits for them, and re-layouts, on_device(): spread, mean = (both[0].reshape(-1), both[1].reshape(-1))  2.64 us

profile of v1, /device:TPU:1, one launch (start us, length us, event | category | flops | bytes accessed | tf_op | source)
XLA Modules:
  0.0 73.5 jit_solution(17301351714198718174)
XLA Ops:
  0.6 0.0 copy-start
  0.6 1.2 %copy-done = bf16[512,1024]{1,0:T(8,128)(2,1)S(1)} copy-done((bf16[512,1024]{1,0:T(8,128)(2,1)S(1)}, bf16[512,1024]{1,0:T(8,128)(2,1)}, u32[]{:S(2)}) %copy-start) | copy-done | bytes 1048600
  1.9 0.0 copy-start.1
  1.9 1.2 %copy-done.1 = bf16[512,1024]{1,0:T(8,128)(2,1)S(1)} copy-done((bf16[512,1024]{1,0:T(8,128)(2,1)S(1)}, bf16[512,1024]{1,0:T(8,128)(2,1)}, u32[]{:S(2)}) %copy-start.1) | copy-done | bytes 1048600
  3.1 0.0 copy-start.2
  3.1 0.9 %copy-done.2 = bf16[512,256]{1,0:T(8,128)(2,1)S(1)} copy-done((bf16[512,256]{1,0:T(8,128)(2,1)S(1)}, bf16[512,256]{1,0:T(8,128)(2,1)}, u32[]{:S(2)}) %copy-start.2) | copy-done | bytes 262168
  4.0 0.0 copy-start.3
  4.0 0.9 %copy-done.3 = bf16[512,256]{1,0:T(8,128)(2,1)S(1)} copy-done((bf16[512,256]{1,0:T(8,128)(2,1)S(1)}, bf16[512,256]{1,0:T(8,128)(2,1)}, u32[]{:S(2)}) %copy-start.3) | copy-done | bytes 262168
  5.0 0.0 copy-start.4
  5.0 0.8 %copy-done.4 = f32[16384]{0:T(1024)S(1)} copy-done((f32[16384]{0:T(1024)S(1)}, f32[16384]{0:T(1024)}, u32[]{:S(2)}) %copy-start.4) | copy-done | bytes 65560
  5.8 0.0 copy-start.5
  5.8 0.8 %copy-done.5 = f32[16384]{0:T(1024)S(1)} copy-done((f32[16384]{0:T(1024)S(1)}, f32[16384]{0:T(1024)}, u32[]{:S(2)}) %copy-start.5) | copy-done | bytes 65560
  6.7 0.0 copy-start.6
  6.7 0.8 %copy-done.6 = f32[16384]{0:T(1024)S(1)} copy-done((f32[16384]{0:T(1024)S(1)}, f32[16384]{0:T(1024)}, u32[]{:S(2)}) %copy-start.6) | copy-done | bytes 65560
  7.5 56.8 %shard_map.111 = (f32[128,128]{1,0:T(8,128)S(1)}, f32[128,128]{1,0:T(8,128)S(1)}, f32[128,128]{1,0:T(8,128)S(1)}, f32[2,2,2,4,2,128,128]{6,5,4,3,2,1,0:T(8,128)}) custom-call(bf16[512,1024]{1,0:T(8,128)(2,1)S(1)} %copy-done, bf16[512,256]{1,0:T(8,128)(2,1)S(1)} %copy-done.2, bf16[512,256]{1,0:T(8,128)(2,1)S(1)} %copy-done.3, ...), custom_call_target="tpu_custom_call" | custom-call | tf_op jit(solution)/shard_map/pallas_call | solution.py:343
  64.3 0.0 copy-start.7
  64.3 2.6 %fusion = (f32[1,2,2,4,2,128,128]{6,5,4,3,2,1,0:T(8,128)S(1)}, f32[1,2,2,4,2,128,128]{6,5,4,3,2,1,0:T(8,128)S(1)}) fusion(f32[2,2,2,4,2,128,128]{6,5,4,3,2,1,0:T(8,128)} %get-tuple-element.11), kind=kLoop, calls=%fused_computation.1 | loop fusion | bytes 8388608 | tf_op jit(solution)/shard_map/slice | solution.py:366
  67.0 0.2 copy-done.7
  67.2 4.4 %add_convert_fusion = bf16[1,524288]{1,0:T(2,128)(2,1)} fusion(f32[1,524288]{1,0:T(1,128)S(1)} %bitcast.15, f32[1,524288]{1,0:T(1,128)S(1)} %bitcast.14, bf16[1,524288]{1,0:T(2,128)(2,1)S(1)} %copy-done.7), kind=kLoop, calls=%fused_computation | loop fusion | flops 2097152 | bytes 6291456 | tf_op jit(solution)/shard_map/convert_element_type | solution.py:367
  71.6 0.6 copy.15
  72.2 0.6 copy.16
  72.9 0.6 copy.17
Async XLA Ops:
  0.6 1.2 %copy-start = (bf16[512,1024]{1,0:T(8,128)(2,1)S(1)}, bf16[512,1024]{1,0:T(8,128)(2,1)}, u32[]{:S(2)}) copy-start(bf16[512,1024]{1,0:T(8,128)(2,1)} %in_first.1) | copy-start | bytes 3145732
  1.9 1.2 %copy-start.1 = (bf16[512,1024]{1,0:T(8,128)(2,1)S(1)}, bf16[512,1024]{1,0:T(8,128)(2,1)}, u32[]{:S(2)}) copy-start(bf16[512,1024]{1,0:T(8,128)(2,1)} %cot_third.1) | copy-start | bytes 3145732
  3.1 0.9 %copy-start.2 = (bf16[512,256]{1,0:T(8,128)(2,1)S(1)}, bf16[512,256]{1,0:T(8,128)(2,1)}, u32[]{:S(2)}) copy-start(bf16[512,256]{1,0:T(8,128)(2,1)} %cot_first.1) | copy-start | bytes 786436
  4.0 0.9 %copy-start.3 = (bf16[512,256]{1,0:T(8,128)(2,1)S(1)}, bf16[512,256]{1,0:T(8,128)(2,1)}, u32[]{:S(2)}) copy-start(bf16[512,256]{1,0:T(8,128)(2,1)} %in_third.1) | copy-start | bytes 786436
  5.0 0.8 %copy-start.4 = (f32[16384]{0:T(1024)S(1)}, f32[16384]{0:T(1024)}, u32[]{:S(2)}) copy-start(f32[16384]{0:T(1024)} %param.12) | copy-start | bytes 196612
  5.8 0.8 %copy-start.5 = (f32[16384]{0:T(1024)S(1)}, f32[16384]{0:T(1024)}, u32[]{:S(2)}) copy-start(f32[16384]{0:T(1024)} %param.13) | copy-start | bytes 196612
  6.7 0.8 %copy-start.6 = (f32[16384]{0:T(1024)S(1)}, f32[16384]{0:T(1024)}, u32[]{:S(2)}) copy-start(f32[16384]{0:T(1024)} %param.14) | copy-start | bytes 196612
  64.3 2.9 %copy-start.7 = (bf16[1,524288]{1,0:T(2,128)(2,1)S(1)}, bf16[1,524288]{1,0:T(2,128)(2,1)}, u32[]{:S(2)}) copy-start(bf16[1,524288]{1,0:T(2,128)(2,1)} %param.15) | copy-start | bytes 3145732

commit v2 on v1

--- a/solution.py
+++ b/solution.py
@@ -25,11 +25,20 @@
 
 def step_kernel(
     sizes,
-    in_first, cot_first, in_third, cot_third, mean_old, prec_old, mom_old,
-    mean_out, prec_out, mom_out, gathered,
-    part, got_c, sum_f, got_f, sum_g, got_g, sum_z, got_z, divisor,
-    c_sems, f_sems, g_sems, z_sems, zz_sems, gg_sems, ff_sems, cc_sems,
+    *refs,
 ):
+    ins, refs = refs[:8], refs[8:]
+    mean_out, prec_out, mom_out, samples = refs[:4]
+    staged, refs = refs[4:12], refs[12:]
+    in_first, cot_first, in_third, cot_third, mean_old, prec_old, mom_old, noise = staged
+    (
+    gathered, part, got_c, sum_f, got_f, sum_g, got_g, sum_z, got_z, divisor,
+    c_sems, f_sems, g_sems, z_sems, zz_sems, gg_sems, ff_sems, cc_sems, in_sems,
+    ) = refs
+    loads = [pltpu.make_async_copy(ins[i], staged[i], in_sems.at[i]) for i in range(8)]
+    for load in loads:
+        load.start()
+
     X, C, Z, Y, S, splits = sizes
     s = S // splits
     gx, mz, my = (lax.axis_index(name) for name in AXES)
@@ -84,10 +93,16 @@
 
     def products(kind, shape):
         cin, mid = in_first.shape[1], cot_first.shape[1]
+        if kind == 0:
+            loads[0].wait()
+            loads[1].wait()
         right = shape(cot_first[...])
         for r in range(0, cin, BLOCK):
             put(kind, 0, contract_rows(shape(in_first[:, r:r + BLOCK]), right), r, 0, mid)
         base = X * C * Z * Y // 2
+        if kind == 0:
+            loads[2].wait()
+            loads[3].wait()
         left = shape(in_third[...])
         for r in range(0, cin, BLOCK):
             put(kind, base, contract_rows(left, shape(cot_third[:, r:r + BLOCK])), 0, r, cin)
@@ -246,11 +261,21 @@
                 link(*ff_link(p, i - 1, j, True)).wait_recv()
                 send(*cc_link(p, i, j))
 
-    def cc_wait(p):
-        nf, mf, ng, mg = outer(p)
-        for i in range(nf):
-            for j in range(ng):
-                link(*cc_link(p, i, j, True)).wait_recv()
+    def cc_wait(p, i):
+        for j in range(outer(p)[2]):
+            link(*cc_link(p, i, j, True)).wait_recv()
+
+    def sample(p, i, j, c):
+        nf, mf, ng, mg = outer(p)
+        split = pieces[p][1]
+        x, y = xy(p, away(mf, nf - i, nf), away(mg, ng - j, ng))
+        for z in range(Z):
+            row = (((x * C + c) * Z + z) * Y + y) * S + split * s
+            at = pl.ds(pl.multiple_of(row * LANES, s * LANES), s * LANES)
+            normal = noise[0, at].astype(jnp.float32).reshape(s, LANES)
+            value = (gathered[1, x, c, z, y, rows_of(p), :]
+                     + gathered[0, x, c, z, y, rows_of(p), :] * normal)
+            samples[0, at] = value.astype(jnp.bfloat16).reshape(s * LANES)
 
     def publish(p, value):
         gathered[pieces[p][0], mx, mc, mz, my, rows_of(p), :] = value
@@ -303,6 +328,8 @@
         f_add(p, halves(p)[0])
     for p in grad:
         f_add(p, halves(p)[1])
+    for load in loads[4:7]:
+        load.wait()
     for p in curv:
         own_curv(p)
     for p in grad:
@@ -317,12 +344,43 @@
         gg_send(p)
     for p in curv:
         cc_send(p)
+    loads[7].wait()
+    same = splits > 1
+    for p in grad:
+        if same:
+            sample(p, 0, 0, mc)
     for p in grad:
         ff_send(p)
+    for p in curv:
+        for i in range(outer(p)[0]):
+            cc_wait(p, i)
+    if same:
+        for p in grad:
+            for j in range(1, outer(p)[2]):
+                sample(p, 0, j, mc)
+        for p in grad:
+            cc_wait(p, 0)
+            for j in range(outer(p)[2]):
+                sample(p, 0, j, other_c)
     for p in grad:
         cc_send(p)
-    for p in curv + grad:
-        cc_wait(p)
+    if same:
+        for p in grad:
+            for i in range(1, outer(p)[0]):
+                for j in range(outer(p)[2]):
+                    sample(p, i, j, mc)
+    for p in grad:
+        for i in range(1 if same else 0, outer(p)[0]):
+            cc_wait(p, i)
+            if same:
+                for j in range(outer(p)[2]):
+                    sample(p, i, j, other_c)
+    if not same:
+        for p in grad:
+            for i in range(outer(p)[0]):
+                for j in range(outer(p)[2]):
+                    for c in range(C):
+                        sample(p, i, j, c)
     for copy in started:
         copy.wait_send()
 
@@ -340,12 +398,16 @@
     def sems(*shape):
         return pltpu.SemaphoreType.DMA((2, n) + shape)
 
-    mean_new, prec_new, mom_new, both = pl.pallas_call(
+    inputs = (in_first, cot_first, in_third, cot_third,
+              *(old.reshape(S, LANES) for old in (mean_old, prec_old, mom_old)), noise)
+    mean_new, prec_new, mom_new, sample_row = pl.pallas_call(
         functools.partial(step_kernel, sizes),
-        out_shape=(shard, shard, shard, jax.ShapeDtypeStruct((2, X, C, Z, Y, S, LANES), jnp.float32)),
-        in_specs=[vmem] * 7,
+        out_shape=(shard, shard, shard, jax.ShapeDtypeStruct(noise.shape, jnp.bfloat16)),
+        in_specs=[pl.BlockSpec(memory_space=pltpu.HBM)] * 8,
         out_specs=[vmem] * 4,
         scratch_shapes=[
+            *(pltpu.VMEM(value.shape, value.dtype) for value in inputs),
+            f32(2, X, C, Z, Y, S),
             f32(2, X, C, Z, Y, S),
             f32(n, X, Z, Y, s),
             f32(n, X * Y, Z, s),
@@ -357,15 +419,13 @@
             f32(S),
             sems(X), sems(X * Y), sems(wide), sems(Z),
             sems(Z), sems(wide * Z), sems(X * Y), sems(X * Y),
+            pltpu.SemaphoreType.DMA((8,)),
         ],
         compiler_params=pltpu.CompilerParams(
-            collective_id=0, has_side_effects=True, vmem_limit_bytes=48 * 1024 * 1024
+            collective_id=0, has_side_effects=True, vmem_limit_bytes=40 * 1024 * 1024
         ),
-    )(in_first, cot_first, in_third, cot_third,
-      *(old.reshape(S, LANES) for old in (mean_old, prec_old, mom_old)))
-    spread, mean = both[0].reshape(-1), both[1].reshape(-1)
-    sample_row = (mean + spread * noise[0].astype(jnp.float32)).astype(jnp.bfloat16)
-    return (mean_new.reshape(-1), prec_new.reshape(-1), mom_new.reshape(-1), sample_row.reshape(1, -1))
+    )(*(pltpu.with_memory_space_constraint(value, pltpu.HBM) for value in inputs))
+    return (mean_new.reshape(-1), prec_new.reshape(-1), mom_new.reshape(-1), sample_row)
 
 
 def solution(mesh):

time: 73.9 us -> 60.3 us (0.82)
  local copies, waits for them, and re-layouts: 11.6 us -> 3.22 us
  other arithmetic: 4.44 us -> 0 us
    unnamed x19 -> x4, local copies, waits for them, and re-layouts: 8.96 us -> 3.22 us
    convert_element_type x1 -> x0, other arithmetic: 4.44 us -> none  [on_device(): (mean + spread * noise[0].astype(jnp.float32)).astype(jnp.bfloat16)]
    slice x1 -> x0, local copies, waits for them, and re-layouts: 2.64 us -> none  [on_device(): spread, mean = (both[0].reshape(-1), both[1].reshape(-1))]
where the time goes in v2:
time: 60.3 us; the launch traced here: 60.2 us
  Pallas kernels  56.3 us (93%)
  local copies, waits for them, and re-layouts  3.22 us (5%)
  between operations  0.64 us (1%)
    pallas_call x1, Pallas kernels, on_device(): pl.pallas_call(functools.partial(step_kernel, sizes), out_shape=(shard, s...  56.3 us
    unnamed x4, local copies, waits for them, and re-layouts  3.22 us

profile of v2, /device:TPU:1, one launch (start us, length us, event | category | flops | bytes accessed | tf_op | source)
XLA Modules:
  0.0 60.2 jit_solution(9890441279908538459)
XLA Ops:
  0.6 56.3 %shard_map.111 = (f32[128,128]{1,0:T(8,128)S(1)}, f32[128,128]{1,0:T(8,128)S(1)}, f32[128,128]{1,0:T(8,128)S(1)}, bf16[1,524288]{1,0:T(2,128)(2,1)S(1)}) custom-call(bf16[512,1024]{1,0:T(8,128)(2,1)} %refs_0_.1, bf16[512,256]{1,0:T(8,128)(2,1)} %refs_1_.1, bf16[512,256]{1,0:T(8,128)(2,1)} %refs_2_.1, bf16[512,1024]{1,0:T(8,128)(2,1)} %refs_3_.1, ...), custom_call_target="tpu_custom_call" | custom-call | tf_op jit(solution)/shard_map/pallas_call | solution.py:403
  57.0 0.6 %copy.16 = f32[16384]{0:T(1024)} copy(f32[16384]{0:T(1024)S(1)} %bitcast.8) | data formatting | bytes 131072
  57.6 0.6 %copy.17 = f32[16384]{0:T(1024)} copy(f32[16384]{0:T(1024)S(1)} %bitcast.7) | data formatting | bytes 131072
  58.2 0.6 %copy.18 = f32[16384]{0:T(1024)} copy(f32[16384]{0:T(1024)S(1)} %bitcast.6) | data formatting | bytes 131072
  58.9 1.3 %copy.19 = bf16[1,524288]{1,0:T(2,128)(2,1)} copy(bf16[1,524288]{1,0:T(2,128)(2,1)S(1)} %get-tuple-element.19) | data formatting | bytes 2097152
